TPU v7x, 32 devices: a whole 2x2x4 slice. The times are simulated.
32 devices in a mesh: pr: 8 (over y, x, core), pc: 4 (over z).
Axes of the slice: x: 2, y: 2, z: 4, core: 2. Of those that a mesh axis runs over, the one named last changes fastest.
Arguments:
- pair_array: bfloat16 [256, 256, 128], P('pr', 'pc'), may hold values from -6 to 6
- left_weight: bfloat16 [128, 128], replicated, may hold values from -0.5 to 0.5
- right_weight: bfloat16 [128, 128], replicated, may hold values from -0.5 to 0.5
- left_gate: bfloat16 [128, 128], replicated, may hold values from -0.5 to 0.5
- right_gate: bfloat16 [128, 128], replicated, may hold values from -0.5 to 0.5
- mid_gain: float32 [128], replicated, may hold values from 0.25 to 1.75
- out_weight: bfloat16 [128, 128], replicated, may hold values from -0.5 to 0.5
- out_gate: bfloat16 [128, 128], replicated, may hold values from -0.5 to 0.5
Outputs:
- pair_update: bfloat16 [256, 256, 128], P('pr', 'pc')
All inputs are finite; a program needn't handle non-finite values.
Results may differ from a plain program's by a relative error of at most 0.012.
Values may be sent and summed in bfloat16 or wider, within the bound.
A program may use at most 128 MiB of HBM per device.

v0:
```python
import jax
import jax.numpy as jnp
from jax import lax
from jax.sharding import PartitionSpec as P


def unit_channels(values, channel_gain):
    centred = values - jnp.mean(values, axis=-1, keepdims=True)
    return (
        centred
        * lax.rsqrt(jnp.mean(centred * centred, axis=-1, keepdims=True) + 1e-05)
        * channel_gain
    )


def make_factors(pair_in, left_weight, right_weight, left_gate, right_gate):
    left = jnp.einsum("ijc,cd->ijd", pair_in, left_weight, preferred_element_type=jnp.float32)
    left = left * jax.nn.sigmoid(
        jnp.einsum("ijc,cd->ijd", pair_in, left_gate, preferred_element_type=jnp.float32)
    )
    right = jnp.einsum("ijc,cd->ijd", pair_in, right_weight, preferred_element_type=jnp.float32)
    right = right * jax.nn.sigmoid(
        jnp.einsum("ijc,cd->ijd", pair_in, right_gate, preferred_element_type=jnp.float32)
    )
    return (pair_in, left.astype(jnp.bfloat16), right.astype(jnp.bfloat16))


def to_pair(mixed, ready, mid_gain, out_weight, out_gate):
    scaled = unit_channels(mixed.astype(jnp.float32), mid_gain).astype(jnp.bfloat16)
    scaled = lax.optimization_barrier(scaled)
    gate = jax.nn.sigmoid(
        jnp.einsum("ijc,cd->ijd", ready, out_gate, preferred_element_type=jnp.float32)
    )
    return (
        jnp.einsum("ijd,dc->ijc", scaled, out_weight, preferred_element_type=jnp.float32) * gate
    ).astype(jnp.bfloat16)


def on_device(
    pair_array, left_weight, right_weight, left_gate, right_gate, mid_gain, out_weight, out_gate
):
    ready, left, right = make_factors(pair_array, left_weight, right_weight, left_gate, right_gate)
    count = pair_array.shape[0] * lax.axis_size("pr")
    left_lines, right_lines = (
        lax.all_to_all(left, "pr", split_axis=2, concat_axis=0, tiled=True),
        lax.all_to_all(right, "pr", split_axis=2, concat_axis=0, tiled=True),
    )
    strip = jnp.einsum(
        "kid,kjd->ijd",
        lax.all_gather(left_lines, "pc", axis=1, tiled=True),
        right_lines,
        preferred_element_type=jnp.float32,
    )
    strip = (strip * count ** (-0.5)).astype(jnp.bfloat16)
    mixed = lax.all_to_all(strip, "pr", split_axis=0, concat_axis=2, tiled=True)
    return to_pair(mixed, ready, mid_gain, out_weight, out_gate)


def solution(mesh):
    return jax.shard_map(
        on_device,
        mesh=mesh,
        in_specs=(P("pr", "pc", None), P(), P(), P(), P(), P(), P(), P()),
        out_specs=P("pr", "pc", None),
        check_vma=False,
    )
```

profile of v0, /device:TPU:0, one launch (start us, length us, event | category | flops | bytes accessed | tf_op | source)
XLA Modules:
  0.0 104.0 jit_solution(1541400130074911763)
XLA Ops:
  6.5 0.0 copy-start
  6.5 0.0 all-gather.2.cloned.1.call-start
  6.5 1.0 copy-done
  7.6 1.0 fusion.24
  8.6 1.2 %fusion.14 = bf16[32,64,128]{2,1,0:T(8,128)(2,1)S(1)} fusion(f32[32,64,128]{2,1,0:T(8,128)S(1)} %fusion.24, bf16[32,64,128]{2,1,0:T(8,128)(2,1)S(1)} %copy-done, bf16[128,128]{1,0:T(8,128)(2,1)} %param.11), kind=kOutput, calls=%fused_computation.22 | convolution fusion | flops 68419584 | bytes 2129920 | tf_op jit(solution)/shard_map/ijc,cd->ijd/dot_general | solution.py:19
  9.8 1.6 %copy.25 = bf16[32,64,128]{1,0,2:T(8,128)(2,1)S(1)} copy(bf16[32,64,128]{2,1,0:T(8,128)(2,1)S(1)} %fusion.14) | data formatting | bytes 1048576 | tf_op jit(solution)/shard_map/convert_element_type | solution.py:25
  11.4 0.7 reshape.28
  12.2 14.7 %all_to_all.45 = bf16[8,2,16384]{2,1,0:T(2,128)(2,1)S(1)} all-to-all(bf16[8,2,16384]{2,1,0:T(2,128)(2,1)S(1)} %reshape.28), channel_id=1, replica_groups=mesh['pr'=8,'pc'=4] {'pr'}, dimensions={0} | all-to-all | bytes 1048576 | tf_op jit(solution)/shard_map/all_to_all | solution.py:45
  26.8 0.7 reshape.29
  27.5 0.0 copy-start.1
  27.5 0.4 copy.27
  27.9 0.0 copy-start.4
  28.0 1.6 %copy.28 = bf16[256,64,16]{0,1,2:T(8,128)(2,1)} copy(bf16[256,64,16]{1,2,0:T(8,128)(2,1)S(1)} %bitcast.66) | data formatting | bytes 1048576 | tf_op jit(solution)/shard_map/all_to_all | solution.py:45
  29.6 0.0 all-gather.2.cloned.1.call-update
  29.6 0.0 copy-done.1
  29.6 0.3 fusion.27
  29.9 0.0 copy-done.4
  29.9 0.4 fusion.15
  30.4 1.6 %copy.22 = bf16[32,64,128]{1,0,2:T(8,128)(2,1)S(1)} copy(bf16[32,64,128]{2,1,0:T(8,128)(2,1)S(1)} %fusion.15) | data formatting | bytes 1048576 | tf_op jit(solution)/shard_map/convert_element_type | solution.py:25
  32.0 0.7 reshape.30
  32.7 12.1 %all_to_all.46 = bf16[8,2,16384]{2,1,0:T(2,128)(2,1)S(1)} all-to-all(bf16[8,2,16384]{2,1,0:T(2,128)(2,1)S(1)} %reshape.30), channel_id=1, replica_groups=mesh['pr'=8,'pc'=4] {'pr'}, dimensions={0} | all-to-all | bytes 1048576 | tf_op jit(solution)/shard_map/all_to_all | solution.py:46
  44.8 0.7 reshape.31
  45.5 0.4 copy.24
  45.9 28.9 %all-gather.2.cloned.1.call-done = bf16[256,256,16]{0,1,2:T(8,128)(2,1)} async-done(((bf16[256,64,16]{0,1,2:T(8,128)(2,1)}), bf16[256,256,16]{0,1,2:T(8,128)(2,1)}) %all-gather.2.cloned.1.call-update) | async-done | bytes 2097168 | tf_op jit(solution)/shard_map/all_gather | solution.py:50
  74.8 2.4 %fusion.18 = bf16[256,64,16]{0,1,2:T(8,128)(2,1)S(1)} fusion(bf16[256,256,16]{0,1,2:T(8,128)(2,1)} %all-gather.2.cloned.1.call-done, bf16[256,64,16]{1,2,0:T(8,128)(2,1)S(1)} %bitcast.61), kind=kOutput, calls=%fused_computation.26 | convolution fusion | flops 134742016 | bytes 3145728 | tf_op jit(solution)/shard_map/kid,kjd->ijd/dot_general | solution.py:48
  77.2 0.0 copy-start.5
  77.2 1.0 copy.30
  78.1 1.5 %reshape.32 = bf16[8,2,16384]{2,1,0:T(2,128)(2,1)} reshape(bf16[256,16,64]{2,1,0:T(8,128)(2,1)S(1)} %bitcast.64) | data formatting | bytes 1048576
  79.6 3.7 %all-to-all-start.2 = ((bf16[8,2,16384]{2,1,0:T(2,128)(2,1)}), bf16[8,2,16384]{2,1,0:T(2,128)(2,1)S(1)}, u32[]{:S(2)}, u32[]{:S(2)}) async-start(bf16[8,2,16384]{2,1,0:T(2,128)(2,1)} %reshape.32), calls=%async_computation.2 | async-start | bytes 1048576 | tf_op jit(solution)/shard_map/all_to_all | solution.py:55
  83.3 0.0 copy-done.5
  83.3 0.4 fusion.13
  83.8 9.3 %all-to-all-done.2 = bf16[8,2,16384]{2,1,0:T(2,128)(2,1)S(1)} async-done(((bf16[8,2,16384]{2,1,0:T(2,128)(2,1)}), bf16[8,2,16384]{2,1,0:T(2,128)(2,1)S(1)}, u32[]{:S(2)}, u32[]{:S(2)}) %all-to-all-start.2) | async-done | bytes 524320 | tf_op jit(solution)/shard_map/all_to_all | solution.py:55
  93.0 0.7 reshape.33
  93.7 0.2 convert_bitcast_fusion
  93.9 0.2 fusion.19
  94.1 0.4 multiply_reduce_fusion
  94.5 0.0 copy-start.3
  94.5 0.3 copy.31
  94.8 0.4 copy-done.3
  95.2 0.0 copy-start.2
  95.2 0.5 fusion.2
  95.6 0.3 copy-done.2
  95.9 1.3 %fusion.17 = bf16[32,64,128]{2,1,0:T(8,128)(2,1)} fusion(f32[32,64,128]{2,1,0:T(8,128)S(1)} %fusion.13, bf16[32,64,128]{1,2,0:T(8,128)(2,1)S(1)} %fusion.2, bf16[128,128]{1,0:T(8,128)(2,1)S(1)} %copy-done.2), kind=kOutput, calls=%fused_computation.25 | convolution fusion | flops 67633152 | bytes 2129920 | tf_op jit(solution)/shard_map/ijd,dc->ijc/dot_general | solution.py:35
  (2 shorter events, 0.0 us)
Async XLA Ops:
  6.5 1.0 %copy-start = (bf16[32,64,128]{2,1,0:T(8,128)(2,1)S(1)}, bf16[32,64,128]{2,1,0:T(8,128)(2,1)}, u32[]{:S(2)}) copy-start(bf16[32,64,128]{2,1,0:T(8,128)(2,1)} %param.8) | copy-start | bytes 1572868
  6.5 68.3 %all-gather.2.cloned.1.call-start = ((), (), s32[]{:S(2)}) async-start(), calls=%async_computation.3 | async-start | bytes 2621440 | tf_op jit(solution)/shard_map/all_gather | solution.py:50
  27.5 2.1 %copy-start.1 = (bf16[128,128]{1,0:T(8,128)(2,1)S(1)}, bf16[128,128]{1,0:T(8,128)(2,1)}, u32[]{:S(2)}) copy-start(bf16[128,128]{1,0:T(8,128)(2,1)} %param.10) | copy-start | bytes 98308
  27.9 2.0 %copy-start.4 = (bf16[128,128]{1,0:T(8,128)(2,1)S(1)}, bf16[128,128]{1,0:T(8,128)(2,1)}, u32[]{:S(2)}) copy-start(bf16[128,128]{1,0:T(8,128)(2,1)} %param.12) | copy-start | bytes 98308
  77.2 6.2 %copy-start.5 = (bf16[128,128]{1,0:T(8,128)(2,1)S(1)}, bf16[128,128]{1,0:T(8,128)(2,1)}, u32[]{:S(2)}) copy-start(bf16[128,128]{1,0:T(8,128)(2,1)} %param.15) | copy-start | bytes 98308
  79.6 13.4 %all-to-all-start.2 = ((bf16[8,2,16384]{2,1,0:T(2,128)(2,1)}), bf16[8,2,16384]{2,1,0:T(2,128)(2,1)S(1)}, u32[]{:S(2)}, u32[]{:S(2)}) async-start(bf16[8,2,16384]{2,1,0:T(2,128)(2,1)} %reshape.32), calls=%async_computation.2 | async-start | bytes 1048576 | tf_op jit(solution)/shard_map/all_to_all | solution.py:55
  94.5 0.7 copy-start.3
  95.2 0.8 copy-start.2
Sparse Core Ops, SparseCore 0:
  29.7 45.0 all-gather.1
where the time goes:
time: 105 us; the launch traced here: 104 us
  waiting for transfers between devices  38.2 us (36%)
  blocking collectives  26.8 us (26%)
  between operations  13.6 us (13%)
  local copies, waits for them, and re-layouts  13.5 us (13%)
  matrix products  6.96 us (7%)
  starting transfers between devices  3.68 us (4%)
  other arithmetic  1.27 us (1%)
    all_gather x1, waiting for transfers between devices, on_device(): lax.all_gather(left_lines, 'pc', axis=1, tiled=True)  28.9 us
    all_to_all x1, blocking collectives, on_device(): lax.all_to_all(left, 'pr', split_axis=2, concat_axis=0, tiled=True)  14.7 us
    all_to_all x1, blocking collectives, on_device(): lax.all_to_all(right, 'pr', split_axis=2, concat_axis=0, tiled=True)  12.1 us
    all_to_all x1, waiting for transfers between devices, on_device(): mixed = lax.all_to_all(strip, 'pr', split_axis=0, concat_axis=2, tiled=True)  9.25 us
    unnamed x18, local copies, waits for them, and re-layouts  6.59 us
    all_to_all x1, starting transfers between devices, on_device(): mixed = lax.all_to_all(strip, 'pr', split_axis=0, concat_axis=2, tiled=True)  3.67 us
    convert_element_type x2, local copies, waits for them, and re-layouts, make_factors(): return (pair_in, left.astype(jnp.bfloat16), right.astype(jnp.bfloat16))  3.24 us
    dot_general x1, matrix products, on_device(): jnp.einsum('kid,kjd->ijd', lax.all_gather(left_lines, 'pc', axis=1, tiled...  2.35 us
  transfers between devices with their start and end apart: 2, of which 2 were waited for; matrix products, arithmetic and copies ran while one was open for 4% of the time, Pallas kernels for 0%

commit v1 on v0

--- a/solution.py
+++ b/solution.py
@@ -2,6 +2,12 @@
 import jax.numpy as jnp
 from jax import lax
 from jax.sharding import PartitionSpec as P
+
+
+def joined_along(blocks, dim):
+    shape = list(blocks.shape[1:])
+    shape[dim] *= blocks.shape[0]
+    return jnp.moveaxis(blocks, 0, dim).reshape(shape)
 
 
 def unit_channels(values, channel_gain):
@@ -45,12 +51,26 @@
         lax.all_to_all(left, "pr", split_axis=2, concat_axis=0, tiled=True),
         lax.all_to_all(right, "pr", split_axis=2, concat_axis=0, tiled=True),
     )
-    strip = jnp.einsum(
-        "kid,kjd->ijd",
-        lax.all_gather(left_lines, "pc", axis=1, tiled=True),
-        right_lines,
-        preferred_element_type=jnp.float32,
-    )
+    devices, position, rows = (lax.axis_size("pc"), lax.axis_index("pc"), left_lines.shape[1])
+    right_2 = [(i, (i + 1) % devices) for i in range(devices)]
+    downward = [(i, (i - 1) % devices) for i in range(devices)]
+    half = devices // 2
+    blocks = {}
+    from_left = from_right = left_lines
+    for lap in range(half + 1):
+        next_left = lax.ppermute(from_left, "pc", right_2) if lap < half else None
+        next_right = lax.ppermute(from_right, "pc", downward) if lap < devices - half - 1 else None
+        blocks[-lap] = jnp.einsum(
+            "kid,kjd->ijd", from_left, right_lines, preferred_element_type=jnp.float32
+        )
+        if 0 < lap < devices - half:
+            blocks[lap] = jnp.einsum(
+                "kid,kjd->ijd", from_right, right_lines, preferred_element_type=jnp.float32
+            )
+        from_left, from_right = (next_left, next_right)
+    blocks = jnp.stack([blocks[k] for k in sorted(blocks)])
+    blocks = blocks[(jnp.arange(devices) - position + half) % devices]
+    strip = joined_along(blocks, 0)
     strip = (strip * count ** (-0.5)).astype(jnp.bfloat16)
     mixed = lax.all_to_all(strip, "pr", split_axis=0, concat_axis=2, tiled=True)
     return to_pair(mixed, ready, mid_gain, out_weight, out_gate)

time: 105 us -> 89.2 us (0.85)
  blocking collectives: 26.8 us -> 0 us
  between operations: 13.6 us -> 0.23 us
  starting transfers between devices: 3.68 us -> 16.4 us
  local copies, waits for them, and re-layouts: 13.5 us -> 18.4 us
  matrix products: 6.96 us -> 11 us
  other arithmetic: 1.27 us -> 4.07 us
    all_gather x1 -> x0, waiting for transfers between devices: 28.9 us -> none  [on_device(): lax.all_gather(left_lines, 'pc', axis=1, tiled=True)]
    all_to_all x2 -> x0, blocking collectives: 26.8 us -> none  [the longest x1 14.7 us: on_device(): lax.all_to_all(left, 'pr', split_axis=2, concat_axis=0, tiled=True)]
    all_to_all x0 -> x2, waiting for transfers between devices: none -> 14.6 us  [the longest x1 8.47 us: on_device(): lax.all_to_all(left, 'pr', split_axis=2, concat_axis=0, tiled=True)]
    ppermute x0 -> x3, waiting for transfers between devices: none -> 14.3 us  [the longest x2 12.8 us: on_device(): next_left = lax.ppermute(from_left, 'pc', right_2) if lap < half else None]
    all_to_all x0 -> x2, starting transfers between devices: none -> 8.68 us  [the longest x1 5.18 us: on_device(): lax.all_to_all(left, 'pr', split_axis=2, concat_axis=0, tiled=True)]
    ppermute x0 -> x3, starting transfers between devices: none -> 3.92 us  [the longest x1 2.29 us: on_device(): lax.ppermute(from_right, 'pc', downward)]
    gather x0 -> x1, local copies, waits for them, and re-layouts: none -> 2.27 us  [on_device(): blocks = blocks[(jnp.arange(devices) - position + half) % devices]]
    dot_general x1 -> x4, matrix products: 2.35 us -> 4.23 us  [the longest x3 2.91 us: on_device(): jnp.einsum('kid,kjd->ijd', from_left, right_lines, preferred_element_type...]
  transfers between devices with their start and end apart: 2 -> 6, of which waited for: 2 -> 6; matrix products, arithmetic and copies ran while one was open for 4% -> 13% of each run, Pallas kernels for 0% -> 0%
where the time goes in v1:
time: 89.2 us; the launch traced here: 88.4 us
  waiting for transfers between devices  38.2 us (43%)
  local copies, waits for them, and re-layouts  18.4 us (21%)
  starting transfers between devices  16.4 us (18%)
  matrix products  11 us (12%)
  other arithmetic  4.07 us (5%)
    ppermute x2, waiting for transfers between devices, on_device(): next_left = lax.ppermute(from_left, 'pc', right_2) if lap < half else None  12.8 us
    all_to_all x1, waiting for transfers between devices, on_device(): mixed = lax.all_to_all(strip, 'pr', split_axis=0, concat_axis=2, tiled=True)  9.28 us
    all_to_all x1, waiting for transfers between devices, on_device(): lax.all_to_all(left, 'pr', split_axis=2, concat_axis=0, tiled=True)  8.47 us
    unnamed x18, local copies, waits for them, and re-layouts  8.19 us
    all_to_all x1, waiting for transfers between devices, on_device(): lax.all_to_all(right, 'pr', split_axis=2, concat_axis=0, tiled=True)  6.09 us
    all_to_all x1, starting transfers between devices, on_device(): lax.all_to_all(left, 'pr', split_axis=2, concat_axis=0, tiled=True)  5.18 us
    all_to_all x1, starting transfers between devices, on_device(): mixed = lax.all_to_all(strip, 'pr', split_axis=0, concat_axis=2, tiled=True)  3.85 us
    all_to_all x1, starting transfers between devices, on_device(): lax.all_to_all(right, 'pr', split_axis=2, concat_axis=0, tiled=True)  3.49 us
  transfers between devices with their start and end apart: 6, of which 6 were waited for; matrix products, arithmetic and copies ran while one was open for 13% of the time, Pallas kernels for 0%

profile of v1, /device:TPU:0, one launch (start us, length us, event | category | flops | bytes accessed | tf_op | source)
XLA Modules:
  0.0 88.4 jit_solution(1121825788342698668)
XLA Ops:
  0.0 0.0 copy-start
  0.0 1.0 %copy-done = bf16[32,64,128]{2,1,0:T(8,128)(2,1)S(1)} copy-done((bf16[32,64,128]{2,1,0:T(8,128)(2,1)S(1)}, bf16[32,64,128]{2,1,0:T(8,128)(2,1)}, u32[]{:S(2)}) %copy-start) | copy-done | bytes 524312
  1.0 1.0 %fusion.21 = f32[32,64,128]{2,1,0:T(8,128)S(1)} fusion(bf16[32,64,128]{2,1,0:T(8,128)(2,1)S(1)} %copy-done, bf16[128,128]{1,0:T(8,128)(2,1)} %param.9), kind=kOutput, calls=%fused_computation.35 | convolution fusion | flops 67108864 | bytes 1605632 | tf_op jit(solution)/shard_map/ijc,cd->ijd/dot_general | solution.py:23
  2.1 1.2 %fusion.14 = bf16[32,64,128]{2,1,0:T(8,128)(2,1)S(1)} fusion(f32[32,64,128]{2,1,0:T(8,128)S(1)} %fusion.21, bf16[32,64,128]{2,1,0:T(8,128)(2,1)S(1)} %copy-done, bf16[128,128]{1,0:T(8,128)(2,1)} %param.11), kind=kOutput, calls=%fused_computation.24 | convolution fusion | flops 68419584 | bytes 2129920 | tf_op jit(solution)/shard_map/ijc,cd->ijd/dot_general | solution.py:25
  3.3 0.0 copy-start.1
  3.3 1.6 %copy.47 = bf16[32,64,128]{1,0,2:T(8,128)(2,1)S(1)} copy(bf16[32,64,128]{2,1,0:T(8,128)(2,1)S(1)} %fusion.14) | data formatting | bytes 1048576 | tf_op jit(solution)/shard_map/convert_element_type | solution.py:31
  4.9 1.5 %reshape.94 = bf16[8,2,16384]{2,1,0:T(2,128)(2,1)} reshape(bf16[128,32,64]{2,1,0:T(8,128)(2,1)S(1)} %bitcast.85) | data formatting | bytes 1048576
  6.4 5.2 %all-to-all-start.1 = ((bf16[8,2,16384]{2,1,0:T(2,128)(2,1)}), bf16[8,2,16384]{2,1,0:T(2,128)(2,1)S(1)}, u32[]{:S(2)}, u32[]{:S(2)}) async-start(bf16[8,2,16384]{2,1,0:T(2,128)(2,1)} %reshape.94), calls=%async_computation.1 | async-start | bytes 1048576 | tf_op jit(solution)/shard_map/all_to_all | solution.py:51
  11.6 0.0 copy-done.1
  11.6 1.2 %fusion.24 = f32[32,64,128]{2,1,0:T(8,128)} fusion(bf16[32,64,128]{2,1,0:T(8,128)(2,1)S(1)} %copy-done, bf16[128,128]{1,0:T(8,128)(2,1)S(1)} %copy-done.1), kind=kOutput, calls=%fused_computation.38 | convolution fusion | flops 67108864 | bytes 1605632 | tf_op jit(solution)/shard_map/ijc,cd->ijd/dot_general | solution.py:27
  12.9 8.5 %all-to-all-done.1 = bf16[8,2,16384]{2,1,0:T(2,128)(2,1)S(1)} async-done(((bf16[8,2,16384]{2,1,0:T(2,128)(2,1)}), bf16[8,2,16384]{2,1,0:T(2,128)(2,1)S(1)}, u32[]{:S(2)}, u32[]{:S(2)}) %all-to-all-start.1) | async-done | bytes 524320 | tf_op jit(solution)/shard_map/all_to_all | solution.py:51
  21.3 0.7 reshape.95
  22.0 0.0 copy-start.4
  22.0 0.4 copy.49
  22.4 0.8 copy.50
  23.3 1.6 %collective-permute-start = (bf16[256,64,16]{0,1,2:T(8,128)(2,1)S(1)}, bf16[256,64,16]{0,1,2:T(8,128)(2,1)}, u32[]{:S(2)}, u32[]{:S(2)}) collective-permute-start(bf16[256,64,16]{0,1,2:T(8,128)(2,1)S(1)} %copy.50), channel_id=1, source_target_pairs={{0,1},{1,2},{2,3},{3,0},{4,5},{5,6},{6,7},{7,4},{8,9},{9,10},{10,1... | collective-permute-start | bytes 1572872 | tf_op jit(solution)/shard_map/ppermute | solution.py:61
  24.9 0.0 copy-done.4
  24.9 1.7 %fusion.15 = bf16[32,64,128]{2,1,0:T(8,128)(2,1)S(1)} fusion(f32[32,64,128]{2,1,0:T(8,128)} %fusion.24, bf16[32,64,128]{2,1,0:T(8,128)(2,1)S(1)} %copy-done, bf16[128,128]{1,0:T(8,128)(2,1)S(1)} %copy-done.4), kind=kOutput, calls=%fused_computation.25 | convolution fusion | flops 68419584 | bytes 2129920 | tf_op jit(solution)/shard_map/ijc,cd->ijd/dot_general | solution.py:29
  26.6 1.6 %copy.44 = bf16[32,64,128]{1,0,2:T(8,128)(2,1)S(1)} copy(bf16[32,64,128]{2,1,0:T(8,128)(2,1)S(1)} %fusion.15) | data formatting | bytes 1048576 | tf_op jit(solution)/shard_map/convert_element_type | solution.py:31
  28.2 1.5 %reshape.92 = bf16[8,2,16384]{2,1,0:T(2,128)(2,1)} reshape(bf16[128,32,64]{2,1,0:T(8,128)(2,1)S(1)} %bitcast.86) | data formatting | bytes 1048576
  29.7 3.5 %all-to-all-start = ((bf16[8,2,16384]{2,1,0:T(2,128)(2,1)}), bf16[8,2,16384]{2,1,0:T(2,128)(2,1)S(1)}, u32[]{:S(2)}, u32[]{:S(2)}) async-start(bf16[8,2,16384]{2,1,0:T(2,128)(2,1)} %reshape.92), calls=%async_computation | async-start | bytes 1048576 | tf_op jit(solution)/shard_map/all_to_all | solution.py:52
  33.2 2.3 %collective-permute-start.2 = (bf16[256,64,16]{0,1,2:T(8,128)(2,1)S(1)}, bf16[256,64,16]{0,1,2:T(8,128)(2,1)}, u32[]{:S(2)}, u32[]{:S(2)}) collective-permute-start(bf16[256,64,16]{0,1,2:T(8,128)(2,1)S(1)} %copy.50), channel_id=1, source_target_pairs={{0,3},{1,0},{2,1},{3,2},{4,7},{5,4},{6,5},{7,6},{8,11},{9,8},{10,9... | collective-permute-start | bytes 1572872 | tf_op jit(solution)/shard_map/ppermute | solution.py:62
  35.5 1.2 %collective-permute-done = bf16[256,64,16]{0,1,2:T(8,128)(2,1)} collective-permute-done((bf16[256,64,16]{0,1,2:T(8,128)(2,1)S(1)}, bf16[256,64,16]{0,1,2:T(8,128)(2,1)}, u32[]{:S(2)}, u32[]{:S(2)}) %collective-permute-start) | collective-permute-done | bytes 524320 | tf_op jit(solution)/shard_map/ppermute | solution.py:61
  36.7 0.0 collective-permute-start.1
  36.7 6.1 %all-to-all-done = bf16[8,2,16384]{2,1,0:T(2,128)(2,1)S(1)} async-done(((bf16[8,2,16384]{2,1,0:T(2,128)(2,1)}), bf16[8,2,16384]{2,1,0:T(2,128)(2,1)S(1)}, u32[]{:S(2)}, u32[]{:S(2)}) %all-to-all-start) | async-done | bytes 524320 | tf_op jit(solution)/shard_map/all_to_all | solution.py:52
  42.8 0.7 reshape.93
  43.5 0.4 copy.46
  43.9 0.8 copy.51
  44.8 0.3 convolution_bitcast_fusion.1
  45.0 1.3 %convolution_bitcast_fusion.2 = f32[1,64,64,16]{1,2,3,0:T(8,128)S(1)} fusion(bf16[256,64,16]{0,1,2:T(8,128)(2,1)S(1)} %copy.51, bf16[256,64,16]{0,1,2:T(8,128)(2,1)} %collective-permute-done), kind=kOutput, calls=%fused_computation.29 | convolution fusion | flops 33554432 | bytes 1310720 | tf_op jit(solution)/shard_map/kid,kjd->ijd/dot_general | solution.py:63
  46.4 1.6 %collective-permute-done.2 = bf16[256,64,16]{0,1,2:T(8,128)(2,1)} collective-permute-done((bf16[256,64,16]{0,1,2:T(8,128)(2,1)S(1)}, bf16[256,64,16]{0,1,2:T(8,128)(2,1)}, u32[]{:S(2)}, u32[]{:S(2)}) %collective-permute-start.2) | collective-permute-done | bytes 524320 | tf_op jit(solution)/shard_map/ppermute | solution.py:62
  47.9 1.3 %convolution_bitcast_fusion = f32[1,64,64,16]{1,2,3,0:T(8,128)S(1)} fusion(bf16[256,64,16]{0,1,2:T(8,128)(2,1)S(1)} %copy.51, bf16[256,64,16]{0,1,2:T(8,128)(2,1)} %collective-permute-done.2), kind=kOutput, calls=%fused_computation.27 | convolution fusion | flops 33554432 | bytes 1310720 | tf_op jit(solution)/shard_map/kid,kjd->ijd/dot_general | solution.py:67
  49.3 11.5 %collective-permute-done.1 = bf16[256,64,16]{0,1,2:T(8,128)(2,1)} collective-permute-done((bf16[256,64,16]{0,1,2:T(8,128)(2,1)}, bf16[256,64,16]{0,1,2:T(8,128)(2,1)}, u32[]{:S(2)}, u32[]{:S(2)}) %collective-permute-start.1) | collective-permute-done | bytes 524320 | tf_op jit(solution)/shard_map/ppermute | solution.py:61
  60.8 1.3 %convolution_bitcast_fusion.3 = f32[1,64,64,16]{1,2,3,0:T(8,128)S(1)} fusion(bf16[256,64,16]{0,1,2:T(8,128)(2,1)S(1)} %copy.51, bf16[256,64,16]{0,1,2:T(8,128)(2,1)} %collective-permute-done.1), kind=kOutput, calls=%fused_computation.30 | convolution fusion | flops 33554432 | bytes 1310720 | tf_op jit(solution)/shard_map/kid,kjd->ijd/dot_general | solution.py:63
  62.1 1.5 %pad_maximum_fusion = f32[4,64,64,16]{1,2,3,0:T(8,128)} fusion(f32[1,64,64,16]{1,2,3,0:T(8,128)S(1)} %convolution_bitcast_fusion, f32[1,64,64,16]{1,2,3,0:T(8,128)S(1)} %convolution_bitcast_fusion.1, f32[1,64,64,16]{1,2,3,0:T(8,128)S(1)} %convolution_bitcast_fusion.2, f32[1,64,64,16]{1,2,3,0:T(8,128)S(1)} %convolution_bitcast_fusion.3), kind=kLoop, calls=%fused_computation.1 | loop fusion | flops 786432 | bytes 2097152 | tf_op jit(solution)/shard_map/stack | solution.py:71
  63.7 2.3 %gather_fusion = f32[4,64,64,16]{1,2,3,0:T(8,128)S(1)} fusion(f32[4,64,64,16]{1,2,3,0:T(8,128)} %pad_maximum_fusion, s32[1024]{0:T(1024)S(1)} %pad_clamp_fusion), kind=kCustom, calls=%fused_computation | custom fusion | bytes 2097168 | tf_op jit(solution)/shard_map/gather | solution.py:72
  65.9 1.2 %multiply_convert_fusion = bf16[4,64,64,16]{1,2,3,0:T(8,128)(2,1)} fusion(f32[4,64,64,16]{1,2,3,0:T(8,128)S(1)} %gather_fusion), kind=kLoop, calls=%fused_computation.8 | loop fusion | flops 524288 | bytes 1572864 | tf_op jit(solution)/shard_map/convert_element_type | solution.py:74
  67.2 0.0 copy-start.5
  67.2 1.9 %copy.64 = bf16[4,64,64,16]{2,3,1,0:T(8,128)(2,1)S(1)} copy(bf16[4,64,64,16]{1,2,3,0:T(8,128)(2,1)} %multiply_convert_fusion) | data formatting | bytes 1048576 | tf_op jit(solution)/shard_map/convert_element_type | solution.py:74
  69.1 1.5 %reshape.96 = bf16[8,2,16384]{2,1,0:T(2,128)(2,1)} reshape(bf16[256,16,64]{2,1,0:T(8,128)(2,1)S(1)} %bitcast.91) | data formatting | bytes 1048576
  70.6 3.8 %all-to-all-start.2 = ((bf16[8,2,16384]{2,1,0:T(2,128)(2,1)}), bf16[8,2,16384]{2,1,0:T(2,128)(2,1)S(1)}, u32[]{:S(2)}, u32[]{:S(2)}) async-start(bf16[8,2,16384]{2,1,0:T(2,128)(2,1)} %reshape.96), calls=%async_computation.2 | async-start | bytes 1048576 | tf_op jit(solution)/shard_map/all_to_all | solution.py:75
  74.5 0.0 copy-done.5
  74.5 0.4 fusion.13
  74.9 9.3 %all-to-all-done.2 = bf16[8,2,16384]{2,1,0:T(2,128)(2,1)S(1)} async-done(((bf16[8,2,16384]{2,1,0:T(2,128)(2,1)}), bf16[8,2,16384]{2,1,0:T(2,128)(2,1)S(1)}, u32[]{:S(2)}, u32[]{:S(2)}) %all-to-all-start.2) | async-done | bytes 524320 | tf_op jit(solution)/shard_map/all_to_all | solution.py:75
  84.2 0.7 reshape.97
  84.8 0.2 convert_bitcast_fusion
  85.0 0.2 fusion.17
  85.3 0.4 multiply_reduce_fusion
  85.7 0.0 copy-start.3
  85.7 0.3 copy.59
  86.0 0.4 copy-done.3
  86.3 0.0 copy-start.2
  86.3 0.5 fusion.2
  86.8 0.3 copy-done.2
  87.1 1.3 %fusion.16 = bf16[32,64,128]{2,1,0:T(8,128)(2,1)} fusion(f32[32,64,128]{2,1,0:T(8,128)S(1)} %fusion.13, bf16[32,64,128]{1,2,0:T(8,128)(2,1)S(1)} %fusion.2, bf16[128,128]{1,0:T(8,128)(2,1)S(1)} %copy-done.2), kind=kOutput, calls=%fused_computation.26 | convolution fusion | flops 67633152 | bytes 2129920 | tf_op jit(solution)/shard_map/ijd,dc->ijc/dot_general | solution.py:41
  (4 shorter events, 0.0 us)
Async XLA Ops:
  0.0 1.0 %copy-start = (bf16[32,64,128]{2,1,0:T(8,128)(2,1)S(1)}, bf16[32,64,128]{2,1,0:T(8,128)(2,1)}, u32[]{:S(2)}) copy-start(bf16[32,64,128]{2,1,0:T(8,128)(2,1)} %param.8) | copy-start | bytes 1572868
  3.3 8.3 %copy-start.1 = (bf16[128,128]{1,0:T(8,128)(2,1)S(1)}, bf16[128,128]{1,0:T(8,128)(2,1)}, u32[]{:S(2)}) copy-start(bf16[128,128]{1,0:T(8,128)(2,1)} %param.10) | copy-start | bytes 98308
  6.4 14.9 %all-to-all-start.1 = ((bf16[8,2,16384]{2,1,0:T(2,128)(2,1)}), bf16[8,2,16384]{2,1,0:T(2,128)(2,1)S(1)}, u32[]{:S(2)}, u32[]{:S(2)}) async-start(bf16[8,2,16384]{2,1,0:T(2,128)(2,1)} %reshape.94), calls=%async_computation.1 | async-start | bytes 1048576 | tf_op jit(solution)/shard_map/all_to_all | solution.py:51
  22.0 2.9 %copy-start.4 = (bf16[128,128]{1,0:T(8,128)(2,1)S(1)}, bf16[128,128]{1,0:T(8,128)(2,1)}, u32[]{:S(2)}) copy-start(bf16[128,128]{1,0:T(8,128)(2,1)} %param.12) | copy-start | bytes 98308
  23.3 13.5 %collective-permute-start = (bf16[256,64,16]{0,1,2:T(8,128)(2,1)S(1)}, bf16[256,64,16]{0,1,2:T(8,128)(2,1)}, u32[]{:S(2)}, u32[]{:S(2)}) collective-permute-start(bf16[256,64,16]{0,1,2:T(8,128)(2,1)S(1)} %copy.50), channel_id=1, source_target_pairs={{0,1},{1,2},{2,3},{3,0},{4,5},{5,6},{6,7},{7,4},{8,9},{9,10},{10,1... | collective-permute-start | bytes 1572872 | tf_op jit(solution)/shard_map/ppermute | solution.py:61
  29.7 13.2 %all-to-all-start = ((bf16[8,2,16384]{2,1,0:T(2,128)(2,1)}), bf16[8,2,16384]{2,1,0:T(2,128)(2,1)S(1)}, u32[]{:S(2)}, u32[]{:S(2)}) async-start(bf16[8,2,16384]{2,1,0:T(2,128)(2,1)} %reshape.92), calls=%async_computation | async-start | bytes 1048576 | tf_op jit(solution)/shard_map/all_to_all | solution.py:52
  33.2 14.7 %collective-permute-start.2 = (bf16[256,64,16]{0,1,2:T(8,128)(2,1)S(1)}, bf16[256,64,16]{0,1,2:T(8,128)(2,1)}, u32[]{:S(2)}, u32[]{:S(2)}) collective-permute-start(bf16[256,64,16]{0,1,2:T(8,128)(2,1)S(1)} %copy.50), channel_id=1, source_target_pairs={{0,3},{1,0},{2,1},{3,2},{4,7},{5,4},{6,5},{7,6},{8,11},{9,8},{10,9... | collective-permute-start | bytes 1572872 | tf_op jit(solution)/shard_map/ppermute | solution.py:62
  36.7 24.1 %collective-permute-start.1 = (bf16[256,64,16]{0,1,2:T(8,128)(2,1)}, bf16[256,64,16]{0,1,2:T(8,128)(2,1)}, u32[]{:S(2)}, u32[]{:S(2)}) collective-permute-start(bf16[256,64,16]{0,1,2:T(8,128)(2,1)} %collective-permute-done), channel_id=1, source_target_pairs={{0,1},{1,2},{2,3},{3,0},{4,5},{5,6},{6,7},{7,4},{8,9},{9,10},{10,1... | collective-permute-start | bytes 1572872 | tf_op jit(solution)/shard_map/ppermute | solution.py:61
  67.2 7.3 %copy-start.5 = (bf16[128,128]{1,0:T(8,128)(2,1)S(1)}, bf16[128,128]{1,0:T(8,128)(2,1)}, u32[]{:S(2)}) copy-start(bf16[128,128]{1,0:T(8,128)(2,1)} %param.15) | copy-start | bytes 98308
  70.6 13.6 %all-to-all-start.2 = ((bf16[8,2,16384]{2,1,0:T(2,128)(2,1)}), bf16[8,2,16384]{2,1,0:T(2,128)(2,1)S(1)}, u32[]{:S(2)}, u32[]{:S(2)}) async-start(bf16[8,2,16384]{2,1,0:T(2,128)(2,1)} %reshape.96), calls=%async_computation.2 | async-start | bytes 1048576 | tf_op jit(solution)/shard_map/all_to_all | solution.py:75
  85.7 0.7 copy-start.3
  86.3 0.8 copy-start.2
